TPU v7x, 256 devices: a whole 4x4x8 slice. The times are simulated.
256 devices in a mesh: dap: 16 (over x, z_lo), cplx: 16 (over y, z_hi, core).
Axes of the slice: x: 4, y: 4, z: 8 (z_hi: 2, z_lo: 4; z = z_hi * 4 + z_lo), core: 2. Of those that a mesh axis runs over, the one named last changes fastest.
Arguments:
- pair: bfloat16 [192, 3072, 128], P('dap', 'cplx'), parts along dimension 1, may hold values from -6 to 6
- cotangent: bfloat16 [192, 3072, 128], P('dap', 'cplx'), parts along dimension 1, may hold values from -6 to 6
- residue_mask: int32 [3072], P('cplx'), parts along dimension 0, may hold values 0 or 1
- chain_ids: int32 [3072], P('cplx'), parts along dimension 0, may hold values from 0 to 2, never falling along the last dimension, each value on 1 to 96 neighbouring positions
- chain_embed: float32 [2, 128], replicated, may hold values from -4 to 4
- out_norm_gain: float32 [128], replicated, may hold values from 0.25 to 1.75
- out_proj: bfloat16 [128, 512], replicated, may hold values from -0.5 to 0.5
- out_gate: bfloat16 [128, 128], replicated, may hold values from -0.5 to 0.5
- out_mid_gain: float32 [128], replicated, may hold values from 0.25 to 1.75
- out_final: bfloat16 [128, 128], replicated, may hold values from -0.5 to 0.5
- in_norm_gain: float32 [128], replicated, may hold values from 0.25 to 1.75
- in_proj: bfloat16 [128, 512], replicated, may hold values from -0.5 to 0.5
- in_gate: bfloat16 [128, 128], replicated, may hold values from -0.5 to 0.5
- in_mid_gain: float32 [128], replicated, may hold values from 0.25 to 1.75
- in_final: bfloat16 [128, 128], replicated, may hold values from -0.5 to 0.5
Outputs:
- pair_grad: bfloat16 [192, 3072, 128], P('dap', 'cplx'), parts along dimension 1
- grad_proj: float32 [2048, 512], P('cplx'), parts along dimension 0
- grad_gate: float32 [2048, 128], P('cplx'), parts along dimension 0
- grad_final: float32 [2048, 128], P('cplx'), parts along dimension 0
- grad_norm_gain: float32 [2048], P('cplx'), parts along dimension 0
- grad_mid_gain: float32 [2048], P('cplx'), parts along dimension 0
There are 16 independent parts, one for each index of `cplx`. A program takes and returns all parts, laid end to end along the dimension named above; an argument that names none is the same for every part. Nothing has to cross between parts.
Inputs may be any that keep to these rules, and one draw needn't show every extreme that they name: `chain_ids`: chain numbers never fall along the residues; each chain has at most 96 residues.
All inputs are finite; a program needn't handle non-finite values.
Results may differ from a plain program's by a relative error of at most 0.019.
Values may be sent and summed in bfloat16 or wider, within the bound.
No kernel may reach another device: no remote copies, remote signals or barrier semaphores. Data moves between devices by JAX's collectives and lax.ppermute only.
A program may use at most 128 MiB of HBM per device.

v0:
```python
import jax
import jax.numpy as jnp
from jax import lax
from jax.sharding import PartitionSpec as P


def together(arrays, axis):
    ends = [0]
    for a in arrays:
        ends.append(ends[-1] + a.size)
    subtotal = lax.psum(jnp.concatenate([a.ravel() for a in arrays]), axis)
    return tuple((subtotal[b:e].reshape(a.shape) for a, b, e in zip(arrays, ends, ends[1:])))


def layer_norm(values_in, gain):
    average = jnp.mean(values_in, axis=-1, keepdims=True)
    centred = values_in - average
    variance = jnp.mean(centred * centred, axis=-1, keepdims=True)
    return centred * lax.rsqrt(variance + 1e-05) * gain


def gated_pair(projected, pair_mask, hidden_width):
    masked = pair_mask[..., None]
    left_act = (
        masked
        * jax.nn.sigmoid(projected[..., :hidden_width])
        * projected[..., hidden_width : 2 * hidden_width]
    )
    right_act = (
        masked
        * jax.nn.sigmoid(projected[..., 2 * hidden_width : 3 * hidden_width])
        * projected[..., 3 * hidden_width :]
    )
    return (left_act, right_act)


def shards(
    pair,
    cotangent,
    residue_mask,
    chain_ids,
    chain_embed,
    out_norm_gain,
    out_proj,
    out_gate,
    out_mid_gain,
    out_final,
    in_norm_gain,
    in_proj,
    in_gate,
    in_mid_gain,
    in_final,
):
    f32 = jnp.float32
    bf16 = jnp.bfloat16
    row_count = pair.shape[0]
    res_count = pair.shape[1]
    hidden_width = out_final.shape[0]
    inv_count = 1.0 / res_count
    row_start = lax.axis_index("dap") * row_count
    row_mask = lax.dynamic_slice_in_dim(residue_mask, row_start, row_count, 0)
    row_chain = lax.dynamic_slice_in_dim(chain_ids, row_start, row_count, 0)
    pair_mask = (row_mask[:, None] * residue_mask[None, :]).astype(f32)
    same_chain = row_chain[:, None] == chain_ids[None, :]
    start = pair.astype(f32) + jnp.where(same_chain[..., None], chain_embed[1], chain_embed[0])
    out_normed = layer_norm(start, out_norm_gain).astype(bf16)
    projected = jnp.dot(out_normed, out_proj, preferred_element_type=f32)
    left_act, right_act = gated_pair(projected, pair_mask, hidden_width)
    left_b = left_act.astype(bf16)
    right_b = right_act.astype(bf16)
    x_out = jnp.einsum(
        "ikc,jkc->ijc",
        left_b,
        lax.all_gather(right_b, "dap", axis=0, tiled=True),
        preferred_element_type=f32,
    )
    y_out = layer_norm(x_out, out_mid_gain).astype(bf16)
    update = jax.nn.sigmoid(jnp.dot(out_normed, out_gate, preferred_element_type=f32)) * jnp.dot(
        y_out, out_final, preferred_element_type=f32
    )
    pair_mid = (start + update).astype(bf16)
    mid_f32 = pair_mid.astype(f32)
    normed_f32, norm_back = jax.vjp(layer_norm, mid_f32, in_norm_gain)
    in_normed = normed_f32.astype(bf16)
    proj_in = jnp.dot(in_normed, in_proj, preferred_element_type=f32)
    (left_in, right_in), glu_back = jax.vjp(
        lambda proj_val: gated_pair(proj_val, pair_mask, hidden_width), proj_in
    )
    left_ib = left_in.astype(bf16)
    right_ib = right_in.astype(bf16)
    columns = lax.all_to_all(left_ib, "dap", split_axis=1, concat_axis=0, tiled=True)
    left_block = columns
    x_in = jnp.einsum(
        "kic,kjc->ijc",
        left_block,
        lax.all_gather(right_ib, "dap", axis=0, tiled=True),
        preferred_element_type=f32,
    )
    y_f32, mid_back = jax.vjp(layer_norm, x_in, in_mid_gain)
    y_in = y_f32.astype(bf16)
    logit = jnp.dot(in_normed, in_gate, preferred_element_type=f32)
    value = jnp.dot(y_in, in_final, preferred_element_type=f32)
    sigma = jax.nn.sigmoid(logit)
    upstream = cotangent.astype(f32)
    grad_value = (upstream * sigma).astype(bf16)
    grad_logit = (upstream * value * sigma * (1.0 - sigma)).astype(bf16)
    grad_final = jnp.einsum("ijc,ijd->cd", y_in, grad_value, preferred_element_type=f32) * inv_count
    grad_gate = (
        jnp.einsum("ijc,ijd->cd", in_normed, grad_logit, preferred_element_type=f32) * inv_count
    )
    grad_y = jnp.dot(grad_value, in_final.T, preferred_element_type=f32)
    grad_x, grad_mid = mid_back(grad_y)
    grad_x_b = grad_x.astype(bf16)
    shard_rows = lax.all_gather(grad_x_b, "dap", axis=0, tiled=True)
    left_block = left_ib
    grad_right = jnp.einsum("kic,ijc->kjc", left_block, shard_rows, preferred_element_type=f32)
    new_block = jnp.einsum("kjc,ijc->kic", right_ib, shard_rows, preferred_element_type=f32)
    grad_p = glu_back((new_block, grad_right))[0].astype(bf16)
    grad_proj = jnp.einsum("ijc,ijd->cd", in_normed, grad_p, preferred_element_type=f32) * inv_count
    grad_normed = jnp.dot(grad_p, in_proj.T, preferred_element_type=f32) + jnp.dot(
        grad_logit, in_gate.T, preferred_element_type=f32
    )
    grad_z, grad_norm = norm_back(grad_normed)
    pair_grad = (upstream + grad_z).astype(bf16)
    reduced = tuple(
        (
            part.astype(jnp.float32)
            for part in together(
                (
                    grad_proj.astype(jnp.bfloat16),
                    grad_gate.astype(jnp.bfloat16),
                    grad_final.astype(jnp.bfloat16),
                    (grad_norm * inv_count).astype(jnp.bfloat16),
                    (grad_mid * inv_count).astype(jnp.bfloat16),
                ),
                "dap",
            )
        )
    )
    return (pair_grad, reduced[0], reduced[1], reduced[2], reduced[3], reduced[4])


def solution(mesh):
    placed = (
        P("dap", "cplx", None),
        P("dap", "cplx", None),
        P("cplx"),
        P("cplx"),
        P(),
        P(),
        P(),
        P(),
        P(),
        P(),
        P(),
        P(),
        P(),
        P(),
        P(),
    )
    return jax.shard_map(
        shards,
        mesh=mesh,
        in_specs=placed,
        out_specs=(
            P("dap", "cplx", None),
            P("cplx", None),
            P("cplx", None),
            P("cplx", None),
            P("cplx"),
            P("cplx"),
        ),
        check_vma=False,
    )
```

profile of v0, /device:TPU:8, one launch (start us, length us, event | category | flops | bytes accessed | tf_op | source)
XLA Modules:
  0.0 931.0 jit_solution(3358620269729586650)
XLA Ops:
  9.6 1.9 fusion.44
  11.6 2.3 multiply_reduce_fusion.4
  15.2 1.5 fusion.31
  16.7 1.9 copy.47
  18.7 2.8 fusion.12
  21.5 204.8 %all-gather.4.cloned.1.call-done = bf16[192,192,128]{2,1,0:T(8,128)(2,1)} async-done(((bf16[12,192,128]{2,1,0:T(8,128)(2,1)}), bf16[192,192,128]{2,1,0:T(8,128)(2,1)}) %all-gather.4.cloned.1.call-update) | async-done | bytes 9437200 | tf_op jit(solution)/shard_map/all_gather | solution.py:74
  226.2 17.4 %copy.46 = bf16[192,192,128]{1,0,2:T(8,128)(2,1)} copy(bf16[192,192,128]{2,1,0:T(8,128)(2,1)} %all-gather.4.cloned.1.call-done) | data formatting | bytes 18874368 | tf_op jit(solution)/shard_map/all_gather | solution.py:74
  243.6 8.2 bitcast_reduce_fusion
  253.8 1.6 convert_reduce_fusion
  257.1 2.0 multiply_convert_fusion.2
  260.7 4.3 all-to-all-start
  266.1 41.9 %all-to-all-done = bf16[12,192,128]{2,0,1:T(8,128)(2,1)} async-done(((bf16[12,192,128]{2,0,1:T(8,128)(2,1)}), bf16[12,192,128]{2,0,1:T(8,128)(2,1)}, u32[]{:S(2)}, u32[]{:S(2)}) %all-to-all-start) | async-done | bytes 589856 | tf_op jit(solution)/shard_map/all_to_all | solution.py:91
  310.2 1.8 copy.53
  312.1 163.0 %all-gather.6.cloned.1.call-done = bf16[192,192,128]{2,1,0:T(8,128)(2,1)} async-done(((bf16[12,192,128]{2,1,0:T(8,128)(2,1)}), bf16[192,192,128]{2,1,0:T(8,128)(2,1)}) %all-gather.6.cloned.1.call-update) | async-done | bytes 9437200 | tf_op jit(solution)/shard_map/all_gather | solution.py:96
  475.0 17.4 %copy.52 = bf16[192,192,128]{1,0,2:T(8,128)(2,1)} copy(bf16[192,192,128]{2,1,0:T(8,128)(2,1)} %all-gather.6.cloned.1.call-done) | data formatting | bytes 18874368 | tf_op jit(solution)/shard_map/all_gather | solution.py:96
  492.4 7.6 fusion.82
  500.1 2.2 copy.54
  504.7 1.7 multiply_reduce_fusion.1
  506.4 2.3 add_convert_fusion.1
  509.1 2.6 copy.59
  511.7 2.6 copy.56
  514.3 2.7 fusion.15
  517.0 198.6 %all-gather.8.cloned.1.call-done = bf16[192,192,128]{2,1,0:T(8,128)(2,1)} async-done(((bf16[12,192,128]{2,1,0:T(8,128)(2,1)}), bf16[192,192,128]{2,1,0:T(8,128)(2,1)}) %all-gather.8.cloned.1.call-update) | async-done | bytes 9437200 | tf_op jit(solution)/shard_map/all_gather | solution.py:114
  715.6 17.4 %copy.55 = bf16[192,192,128]{1,0,2:T(8,128)(2,1)} copy(bf16[192,192,128]{2,1,0:T(8,128)(2,1)} %all-gather.8.cloned.1.call-done) | data formatting | bytes 18874368 | tf_op jit(solution)/shard_map/all_gather | solution.py:114
  733.0 9.5 %fusion.84 = f32[128,192,12]{1,2,0:T(8,128)} fusion(bf16[192,192,128]{1,0,2:T(8,128)(2,1)} %copy.55, bf16[12,192,128]{1,0,2:T(8,128)(2,1)} %copy.59), kind=kOutput, calls=%fused_computation.145 | convolution fusion | flops 113246208 | bytes 11206656 | tf_op jit(solution)/shard_map/kjc,ijc->kic/dot_general | solution.py:117
  742.5 2.7 copy.60
  745.2 7.9 fusion.83
  753.1 2.7 copy.57
  755.8 3.7 bitcast_multiply_fusion.3
  764.8 1.7 fusion.18
  767.7 2.5 fusion.22
  770.2 149.9 %all-reduce.6.cloned.1.call-done = bf16[98560]{0:T(1024)(128)(2,1)} async-done(((bf16[98560]{0:T(1024)(128)(2,1)}), bf16[98560]{0:T(1024)(128)(2,1)}) %all-reduce.6.cloned.1.call-update) | async-done | bytes 197136 | tf_op jit(solution)/shard_map/psum | solution.py:11
  (90 shorter events, 25.6 us)
Async XLA Ops:
  7.2 249.1 %copy-start = (bf16[128,512]{1,0:T(8,128)(2,1)S(1)}, bf16[128,512]{1,0:T(8,128)(2,1)}, u32[]{:S(2)}) copy-start(bf16[128,512]{1,0:T(8,128)(2,1)} %param.26) | copy-start | bytes 393220
  7.2 6.9 copy-start.5
  7.2 6.7 copy-start.16
  7.2 6.8 copy-start.18
  7.2 6.8 copy-start.11
  7.2 219.0 %all-gather.4.cloned.1.call-start = ((), (), s32[]{:S(2)}) async-start(), calls=%async_computation.1 | async-start | bytes 10027008 | tf_op jit(solution)/shard_map/all_gather | solution.py:74
  16.7 2.0 copy-start.19
  16.7 458.3 %all-gather.6.cloned.1.call-start = ((), (), s32[]{:S(2)}) async-start(), calls=%async_computation.2 | async-start | bytes 10027008 | tf_op jit(solution)/shard_map/all_gather | solution.py:96
  251.8 0.7 copy-start.17
  252.5 1.3 copy-start.8
  252.5 1.3 copy-start.12
  253.8 2.5 copy-start.15
  257.1 2.3 copy-start.1
  259.4 1.3 copy-start.6
  259.4 5.8 copy-start.13
  260.7 47.2 %all-to-all-start = ((bf16[12,192,128]{2,0,1:T(8,128)(2,1)}), bf16[12,192,128]{2,0,1:T(8,128)(2,1)}, u32[]{:S(2)}, u32[]{:S(2)}) async-start(bf16[12,192,128]{2,0,1:T(8,128)(2,1)} %copy.49), calls=%async_computation | async-start | bytes 1572864 | tf_op jit(solution)/shard_map/all_to_all | solution.py:91
  265.0 450.6 %all-gather.8.cloned.1.call-start = ((), (), s32[]{:S(2)}) async-start(), calls=%async_computation.3 | async-start | bytes 10027008 | tf_op jit(solution)/shard_map/all_gather | solution.py:114
  502.3 1.1 copy-start.2
  502.3 1.1 copy-start.10
  502.3 1.0 copy-start.14
  508.8 411.3 %all-reduce.6.cloned.1.call-start = ((), (), s32[]{:S(2)}) async-start(), calls=%async_computation.4 | async-start | bytes 397312 | tf_op jit(solution)/shard_map/psum | solution.py:11
  760.8 1.1 copy-start.7
  761.6 1.2 copy-start.3
  764.8 2.9 copy-start.4
  767.0 0.7 copy-start.9
Sparse Core Ops, SparseCore 0:
  16.8 209.3 all-gather.3
  259.5 215.4 all-gather.5
  508.9 206.6 all-gather.7
  767.8 152.2 all-reduce.5
where the time goes:
time: 933 us; the launch traced here: 931 us
  waiting for transfers between devices  758 us (81%)
  local copies, waits for them, and re-layouts  78.5 us (8%)
  matrix products  49.2 us (5%)
  other arithmetic  26.1 us (3%)
  between operations  14.2 us (2%)
    all_gather x1, waiting for transfers between devices, shards(): lax.all_gather(right_b, 'dap', axis=0, tiled=True)  205 us
    all_gather x1, waiting for transfers between devices, shards(): shard_rows = lax.all_gather(grad_x_b, 'dap', axis=0, tiled=True)  199 us
    all_gather x1, waiting for transfers between devices, shards(): lax.all_gather(right_ib, 'dap', axis=0, tiled=True)  163 us
    psum x1, waiting for transfers between devices, together(): subtotal = lax.psum(jnp.concatenate([a.ravel() for a in arrays]), axis)  150 us
    all_to_all x1, waiting for transfers between devices, shards(): lax.all_to_all(left_ib, 'dap', split_axis=1, concat_axis=0, tiled=True)  41.9 us
  transfers between devices with their start and end apart: 5, of which 5 were waited for; matrix products, arithmetic and copies ran while one was open for 2% of the time, Pallas kernels for 0%

commit v1 on v0

--- a/solution.py
+++ b/solution.py
@@ -8,7 +8,9 @@
     ends = [0]
     for a in arrays:
         ends.append(ends[-1] + a.size)
-    subtotal = lax.psum(jnp.concatenate([a.ravel() for a in arrays]), axis)
+    block = jnp.concatenate([a.ravel() for a in arrays])
+    parts = lax.all_gather(block, axis)
+    subtotal = jnp.sum(parts, axis=0)
     return tuple((subtotal[b:e].reshape(a.shape) for a, b, e in zip(arrays, ends, ends[1:])))
 
 

time: 933 us -> 938 us (level)
  other arithmetic: 26.1 us -> 41.1 us
  waiting for transfers between devices: 758 us -> 748 us
    psum x1 -> x0, waiting for transfers between devices: 150 us -> none  [together(): subtotal = lax.psum(jnp.concatenate([a.ravel() for a in arrays]), axis)]
    all_gather x0 -> x1, waiting for transfers between devices: none -> 140 us  [together(): parts = lax.all_gather(block, axis)]
    reduce_sum x0 -> x1, other arithmetic: none -> 17.4 us  [together(): subtotal = jnp.sum(parts, axis=0)]
where the time goes in v1:
time: 938 us; the launch traced here: 936 us
  waiting for transfers between devices  748 us (80%)
  local copies, waits for them, and re-layouts  78.8 us (8%)
  matrix products  49.3 us (5%)
  other arithmetic  41.1 us (4%)
  between operations  14.2 us (2%)
    all_gather x1, waiting for transfers between devices, shards(): lax.all_gather(right_b, 'dap', axis=0, tiled=True)  205 us
    all_gather x1, waiting for transfers between devices, shards(): shard_rows = lax.all_gather(grad_x_b, 'dap', axis=0, tiled=True)  199 us
    all_gather x1, waiting for transfers between devices, shards(): lax.all_gather(right_ib, 'dap', axis=0, tiled=True)  163 us
    all_gather x1, waiting for transfers between devices, together(): parts = lax.all_gather(block, axis)  140 us
    all_to_all x1, waiting for transfers between devices, shards(): lax.all_to_all(left_ib, 'dap', split_axis=1, concat_axis=0, tiled=True)  41.9 us
  transfers between devices with their start and end apart: 5, of which 5 were waited for; matrix products, arithmetic and copies ran while one was open for 2% of the time, Pallas kernels for 0%

profile of v1, /device:TPU:8, one launch (start us, length us, event | category | flops | bytes accessed | tf_op | source)
XLA Modules:
  0.0 936.1 jit_solution(15914234314161798681)
XLA Ops:
  9.6 1.9 fusion.44
  11.6 2.3 multiply_reduce_fusion.4
  16.7 2.0 copy.47
  18.7 2.8 fusion.12
  21.5 204.7 %all-gather.7.cloned.1.call-done = bf16[192,192,128]{2,1,0:T(8,128)(2,1)} async-done(((bf16[12,192,128]{2,1,0:T(8,128)(2,1)}), bf16[192,192,128]{2,1,0:T(8,128)(2,1)}) %all-gather.7.cloned.1.call-update) | async-done | bytes 9437200 | tf_op jit(solution)/shard_map/all_gather | solution.py:76
  226.2 17.4 %copy.46 = bf16[192,192,128]{1,0,2:T(8,128)(2,1)} copy(bf16[192,192,128]{2,1,0:T(8,128)(2,1)} %all-gather.7.cloned.1.call-done) | data formatting | bytes 18874368 | tf_op jit(solution)/shard_map/all_gather | solution.py:76
  243.7 8.2 bitcast_reduce_fusion
  253.8 1.6 convert_reduce_fusion
  257.1 2.0 multiply_convert_fusion.2
  260.7 4.3 all-to-all-start
  266.1 41.9 %all-to-all-done = bf16[12,192,128]{2,0,1:T(8,128)(2,1)} async-done(((bf16[12,192,128]{2,0,1:T(8,128)(2,1)}), bf16[12,192,128]{2,0,1:T(8,128)(2,1)}, u32[]{:S(2)}, u32[]{:S(2)}) %all-to-all-start) | async-done | bytes 589856 | tf_op jit(solution)/shard_map/all_to_all | solution.py:93
  310.2 1.8 copy.53
  312.0 163.0 %all-gather.9.cloned.1.call-done = bf16[192,192,128]{2,1,0:T(8,128)(2,1)} async-done(((bf16[12,192,128]{2,1,0:T(8,128)(2,1)}), bf16[192,192,128]{2,1,0:T(8,128)(2,1)}) %all-gather.9.cloned.1.call-update) | async-done | bytes 9437200 | tf_op jit(solution)/shard_map/all_gather | solution.py:98
  475.0 17.4 %copy.52 = bf16[192,192,128]{1,0,2:T(8,128)(2,1)} copy(bf16[192,192,128]{2,1,0:T(8,128)(2,1)} %all-gather.9.cloned.1.call-done) | data formatting | bytes 18874368 | tf_op jit(solution)/shard_map/all_gather | solution.py:98
  492.4 7.7 fusion.82
  500.1 2.2 copy.54
  504.7 1.7 multiply_reduce_fusion.1
  506.4 2.3 add_convert_fusion.1
  509.0 2.6 copy.59
  511.7 2.6 copy.56
  514.3 2.7 fusion.15
  517.0 198.6 %all-gather.11.cloned.1.call-done = bf16[192,192,128]{2,1,0:T(8,128)(2,1)} async-done(((bf16[12,192,128]{2,1,0:T(8,128)(2,1)}), bf16[192,192,128]{2,1,0:T(8,128)(2,1)}) %all-gather.11.cloned.1.call-update) | async-done | bytes 9437200 | tf_op jit(solution)/shard_map/all_gather | solution.py:116
  715.6 17.4 %copy.55 = bf16[192,192,128]{1,0,2:T(8,128)(2,1)} copy(bf16[192,192,128]{2,1,0:T(8,128)(2,1)} %all-gather.11.cloned.1.call-done) | data formatting | bytes 18874368 | tf_op jit(solution)/shard_map/all_gather | solution.py:116
  733.0 9.5 %fusion.84 = f32[128,192,12]{1,2,0:T(8,128)} fusion(bf16[192,192,128]{1,0,2:T(8,128)(2,1)} %copy.55, bf16[12,192,128]{1,0,2:T(8,128)(2,1)} %copy.59), kind=kOutput, calls=%fused_computation.145 | convolution fusion | flops 113246208 | bytes 11206656 | tf_op jit(solution)/shard_map/kjc,ijc->kic/dot_general | solution.py:119
  742.5 2.7 copy.60
  745.2 7.9 fusion.83
  753.1 2.7 copy.57
  755.8 3.7 bitcast_multiply_fusion.3
  764.8 1.7 fusion.18
  768.0 2.5 fusion.22
  770.5 139.7 %all-gather.13.cloned.1.call-done = bf16[16,1,98560]{2,1,0:T(2,128)(2,1)} async-done(((bf16[1,1,98560]{2,1,0:T(2,128)(2,1)}), bf16[16,1,98560]{2,1,0:T(2,128)(2,1)}) %all-gather.13.cloned.1.call-update) | async-done | bytes 3153936 | tf_op jit(solution)/shard_map/all_gather | solution.py:12
  910.2 17.4 %reduce_sum.176 = bf16[98560]{0:T(1024)(128)(2,1)S(1)} reduce(bf16[16,1,98560]{2,1,0:T(2,128)(2,1)} %all-gather.13.cloned.1.call-done, bf16[]{:T(256)} %constant.38.clone.1), dimensions={0,1}, to_apply=%region_14.15 | reduce | flops 1478400 | bytes 3351042 | tf_op jit(solution)/shard_map/reduce_sum | solution.py:13
  (90 shorter events, 25.0 us)
Async XLA Ops:
  7.2 249.1 %copy-start = (bf16[128,512]{1,0:T(8,128)(2,1)S(1)}, bf16[128,512]{1,0:T(8,128)(2,1)}, u32[]{:S(2)}) copy-start(bf16[128,512]{1,0:T(8,128)(2,1)} %param.26) | copy-start | bytes 393220
  7.2 6.9 copy-start.5
  7.2 6.7 copy-start.15
  7.2 6.8 copy-start.17
  7.2 6.8 copy-start.10
  7.2 219.0 %all-gather.7.cloned.1.call-start = ((), (), s32[]{:S(2)}) async-start(), calls=%async_computation.1 | async-start | bytes 10027008 | tf_op jit(solution)/shard_map/all_gather | solution.py:76
  16.7 2.0 copy-start.18
  16.7 458.3 %all-gather.9.cloned.1.call-start = ((), (), s32[]{:S(2)}) async-start(), calls=%async_computation.2 | async-start | bytes 10027008 | tf_op jit(solution)/shard_map/all_gather | solution.py:98
  251.8 0.7 copy-start.16
  252.5 1.3 copy-start.8
  252.5 1.3 copy-start.11
  253.8 2.5 copy-start.14
  257.1 2.3 copy-start.1
  259.4 1.3 copy-start.6
  259.4 5.8 copy-start.12
  260.7 47.2 %all-to-all-start = ((bf16[12,192,128]{2,0,1:T(8,128)(2,1)}), bf16[12,192,128]{2,0,1:T(8,128)(2,1)}, u32[]{:S(2)}, u32[]{:S(2)}) async-start(bf16[12,192,128]{2,0,1:T(8,128)(2,1)} %copy.49), calls=%async_computation | async-start | bytes 1572864 | tf_op jit(solution)/shard_map/all_to_all | solution.py:93
  265.0 450.6 %all-gather.11.cloned.1.call-start = ((), (), s32[]{:S(2)}) async-start(), calls=%async_computation.3 | async-start | bytes 10027008 | tf_op jit(solution)/shard_map/all_gather | solution.py:116
  502.3 1.1 copy-start.2
  502.3 1.1 copy-start.9
  502.3 1.0 copy-start.13
  508.8 401.4 %all-gather.13.cloned.1.call-start = ((), (), s32[]{:S(2)}) async-start(), calls=%async_computation.4 | async-start | bytes 6702080 | tf_op jit(solution)/shard_map/all_gather | solution.py:12
  760.8 1.1 copy-start.7
  761.6 1.2 copy-start.3
  764.8 3.2 copy-start.4
Sparse Core Ops, SparseCore 0:
  16.8 209.3 all-gather.6
  259.5 215.4 all-gather.8
  508.9 206.6 all-gather.10
  768.1 142.0 all-gather.12
